TPU v7x, 256 devices: a whole 4x4x8 slice. The times are simulated.
256 devices in a mesh: gx: 4 (over y), gy: 8 (over x, core), gz: 8 (over z).
Axes of the slice: x: 4, y: 4, z: 8, core: 2. Of those that a mesh axis runs over, the one named last changes fastest.
Arguments:
- flow_state: float32 [5, 256, 128, 512], P(None, 'gz', 'gy', 'gx'), may hold values from -5 to 120, as said below
- advection: float32 [3, 5], replicated, may hold values from -400 to 400, as said below
- inverse_x: float32 [5, 128, 128], replicated, may hold values from -1 to 1, as said below
- inverse_y: float32 [5, 16, 16], replicated, may hold values from -1 to 1, as said below
- inverse_z: float32 [5, 32, 32], replicated, may hold values from -1 to 1, as said below
- reduced_x: float32 [5, 16, 16], replicated, as said below
- reduced_y: float32 [5, 32, 32], replicated, as said below
- reduced_z: float32 [5, 32, 32], replicated, as said below
Outputs:
- update: float32 [5, 256, 128, 512], P(None, 'gz', 'gy', 'gx')
- rms_norm: float32 [5], replicated
Inputs may be any that keep to these rules, and one draw needn't show every extreme that they name: flow_state[0] (density) lies between 0.5 and 2, and flow_state[4] / density minus half the squared velocity is at least 0.6 in every cell. `advection`: every entry has magnitude between 100 and 400. inverse_x[v] is the inverse of the 128 x 128 matrix with 4 on the diagonal, advection[0, v] / 2 - 2 just above it, -advection[0, v] / 2 - 2 just below it and 0.5 two places off it. inverse_y[v] is the inverse of the 16 x 16 matrix built likewise from advection[1, v]. inverse_z[v] is the inverse of the 32 x 32 matrix built likewise from advection[2, v]. reduced_x[v] is the inverse of I + K, K being the boundary rows and columns of the block inverses times the coupling between blocks, so that S_x equals the exact solution of the banded system along whole x lines with nothing beyond the grid's ends. reduced_y[v] is built likewise for y lines. reduced_z[v] is built likewise for z lines.
All inputs are finite; a program needn't handle non-finite values.
Results may differ from a plain program's by a relative error of at most 0.0002.
Values sent between devices are 32-bit elements.
No kernel may reach another device: no remote copies, remote signals or barrier semaphores. Data moves between devices by JAX's collectives and lax.ppermute only.
A program may use at most 64 MiB of HBM per device.

v0:
```python
import jax
import jax.numpy as jnp
import numpy as np
from jax import lax
from jax.sharding import Mesh
from jax.sharding import PartitionSpec as P

GX_GY_GZ = ("gx", "gy_0", "gy_1", "gz")
GY = ("gy_0", "gy_1")


exact_mode = lax.Precision.HIGHEST
gas_ratio = 0.4
courant = 8000.0
damping = 0.0625
fourth_coef = 0.5


def padded_2(shard, sides, width):
    edges = {}
    for axis, dim in sides:
        devices, length = (lax.axis_size(axis), shard.shape[dim])
        up = [(i, (i + 1) % devices) for i in range(devices)]
        last = lax.slice_in_dim(shard, length - width, length, axis=dim)
        first = lax.slice_in_dim(shard, 0, width, axis=dim)
        edges[dim] = (
            lax.ppermute(last, axis, up),
            lax.ppermute(first, axis, [(b, a) for a, b in up]),
        )
    done = []
    for _, dim in sides:
        low, high = edges[dim]
        around = [(width, width) if d in done else (0, 0) for d in range(shard.ndim)]
        shard = jnp.concatenate([jnp.pad(low, around), shard, jnp.pad(high, around)], axis=dim)
        done.append(dim)
    return shard


def collected_together(shard, axis):
    leaves = jax.tree.leaves(shard)
    turns = sorted(range(len(leaves)), key=lambda k: -leaves[k].size)
    width = (1, *leaves[turns[0]].shape)[-1]
    lines = [
        jnp.pad(leaves[k].reshape(-1), (0, -leaves[k].size % width)).reshape(-1, width)
        for k in turns
    ]
    both, at, found = (lax.all_gather(jnp.concatenate(lines), axis), 0, {})
    for k, line in zip(turns, lines):
        section = both[:, at : at + len(line)].reshape(len(both), -1)
        found[k] = section[:, : leaves[k].size].reshape(-1, *leaves[k].shape)
        at += len(line)
    numbers = iter(range(len(leaves)))
    return jax.tree.map(lambda _: found[next(numbers)], shard)


def combined_by_axis(shard, axes, combine):
    for axis in axes:
        pieces = collected_together(shard, axis)
        shard = jax.tree.map(lambda part: part[0], pieces)
        for k in range(1, lax.axis_size(axis)):
            shard = combine(shard, jax.tree.map(lambda part: part[k], pieces))
    return shard


def in_order(parts, dim):
    parts = jnp.moveaxis(parts, 0, dim)
    dims = parts.shape
    return parts.reshape(*dims[:dim], dims[dim] * dims[dim + 1], *dims[dim + 2 :])


def from_everyone(shard, axis):
    devices = lax.axis_size(axis)
    return lax.all_to_all(
        jnp.broadcast_to(shard[None], (devices, *shard.shape)), axis, 0, 0, tiled=True
    )


def gathered_copies(shard, axis, dim):
    return in_order(from_everyone(shard, axis), dim)


def primitives(flow_state):
    density = flow_state[0]
    velocity = flow_state[1:4] / density
    kinetic = 0.5 * jnp.sum(velocity * velocity, axis=0)
    internal = jnp.maximum(flow_state[4] / density - kinetic, 0.25)
    pressure = gas_ratio * density * internal
    return (velocity, internal, pressure)


def fluxes_along(flow_state, direction):
    velocity, internal, pressure = primitives(flow_state)
    carried = velocity[direction]
    columns = [flow_state[1 + direction]]
    for component in range(3):
        moment = flow_state[1 + component] * carried
        if component == direction:
            moment = moment + pressure
        columns.append(moment)
    columns.append((flow_state[4] + pressure) * carried)
    return jnp.stack(columns)


def window(padded, line_axis, offset, margin):
    slices = [slice(None), slice(2, -2), slice(2, -2), slice(2, -2)]
    extent = padded.shape[line_axis] - 4
    slices[line_axis] = slice(2 + offset - margin, 2 + offset + extent + margin)
    return padded[tuple(slices)]


def residual_field(padded):
    centre = window(padded, 1, 0, 0)
    running = jnp.zeros_like(centre)
    for direction in range(3):
        line_axis = 3 - direction
        fluxes = fluxes_along(window(padded, line_axis, 0, 1), direction)
        extent = fluxes.shape[line_axis]
        forward = lax.slice_in_dim(fluxes, 2, extent, axis=line_axis)
        backward = lax.slice_in_dim(fluxes, 0, extent - 2, axis=line_axis)
        running = running - 0.5 * (forward - backward)
        fourth = (
            window(padded, line_axis, -2, 0)
            - 4.0 * window(padded, line_axis, -1, 0)
            + 6.0 * centre
            - 4.0 * window(padded, line_axis, 1, 0)
            + window(padded, line_axis, 2, 0)
        )
        running = running - damping * fourth
    return running


def combine_stats(first, second):
    return (jnp.maximum(first[0], second[0]), first[1] + second[1])


def neighbour_table(reduced):
    blocks = reduced.shape[1] // 4
    padded = jnp.pad(reduced, ((0, 0), (2, 2), (0, 0)))
    picked = (4 * np.arange(blocks)[:, None] + np.array([0, 1, 6, 7])[None, :]).reshape(-1)
    return jnp.transpose(padded[:, picked, :], (1, 0, 2))


def gather_terms(own_rows, carry, piece):
    columns = lax.slice_in_dim(own_rows, 0, piece.shape[1], axis=2)
    return carry + jnp.einsum("rvq,vqn->rvn", columns, piece, precision=exact_mode)


def empty_rows(boundary_rows):
    return jnp.zeros((4, boundary_rows.shape[0], boundary_rows.shape[2]), jnp.float32)


def line_solve(line_field, line_axis, inverse, speeds, nearby):
    block_len = inverse.shape[1]
    patterns = {3: "vij,vzyj->vzyi", 2: "vij,vzjx->vzix", 1: "vij,vjyx->viyx"}
    local_part = jnp.einsum(patterns[line_axis], inverse, line_field, precision=exact_mode)
    boundary = jnp.concatenate(
        [
            lax.slice_in_dim(local_part, 0, 2, axis=line_axis),
            lax.slice_in_dim(local_part, block_len - 2, block_len, axis=line_axis),
        ],
        axis=line_axis,
    )
    boundary_rows = jnp.moveaxis(boundary, line_axis, 1)
    boundary_rows = boundary_rows.reshape(boundary_rows.shape[0], 4, -1)
    nearby_rows = nearby(boundary_rows)
    flat_shape = list(line_field.shape)
    flat_shape[line_axis] = 1
    pieces = [nearby_rows[position].reshape(flat_shape) for position in range(4)]
    factor = speeds.reshape(-1, 1, 1, 1)
    lower_one = -0.5 * factor - 4.0 * fourth_coef
    upper_one = 0.5 * factor - 4.0 * fourth_coef
    left_first = fourth_coef * pieces[0] + lower_one * pieces[1]
    left_second = fourth_coef * pieces[1]
    right_first = fourth_coef * pieces[2]
    right_second = upper_one * pieces[2] + fourth_coef * pieces[3]
    column_shape = [inverse.shape[0], 1, 1, 1]
    column_shape[line_axis] = block_len

    def column(place):
        return inverse[:, :, place].reshape(column_shape)

    correction = (
        column(0) * left_first
        + column(1) * left_second
        + column(block_len - 2) * right_first
        + column(block_len - 1) * right_second
    )
    return local_part - correction


def shards(flow_state, advection, inverse_x, inverse_y, inverse_z, reduced_x, reduced_y, reduced_z):
    velocity, internal, pressure = primitives(flow_state)
    wave_speed = jnp.sum(jnp.abs(velocity), axis=0) + jnp.sqrt(3.0 * 1.4 * gas_ratio * internal)
    local_top = jnp.max(wave_speed)
    padded = padded_2(flow_state, (("gx", 3), (GY, 2), ("gz", 1)), 2)
    residual = residual_field(padded)
    local_sums = jnp.sum(residual * residual, axis=(1, 2, 3))
    top_speed, squares = combined_by_axis((local_top, local_sums), GX_GY_GZ, combine_stats)
    cell_count = (
        residual.shape[1]
        * residual.shape[2]
        * residual.shape[3]
        * lax.axis_size("gx")
        * lax.axis_size(GY)
        * lax.axis_size("gz")
    )
    rms_norm = jnp.sqrt(squares / float(cell_count))
    time_step = courant / top_speed
    table_x = neighbour_table(reduced_x)
    table_y = neighbour_table(reduced_y)
    table_z = neighbour_table(reduced_z)
    index_x = lax.axis_index("gx")
    index_y = lax.axis_index(GY)
    index_z = lax.axis_index("gz")

    def nearby_x(boundary_rows):
        own_rows = lax.dynamic_slice_in_dim(table_x, 4 * index_x, 4, 0)
        return gather_terms(
            own_rows, empty_rows(boundary_rows), gathered_copies(boundary_rows, "gx", 1)
        )

    def nearby_y(boundary_rows):
        own_rows = lax.dynamic_slice_in_dim(table_y, 4 * index_y, 4, 0)
        return gather_terms(
            own_rows, empty_rows(boundary_rows), gathered_copies(boundary_rows, GY, 1)
        )

    def nearby_z(boundary_rows):
        own_rows = lax.dynamic_slice_in_dim(table_z, 4 * index_z, 4, 0)
        return gather_terms(
            own_rows, empty_rows(boundary_rows), gathered_copies(boundary_rows, "gz", 1)
        )

    line_field = residual
    line_field = line_solve(line_field, 3, inverse_x, advection[0], nearby_x)
    line_field = line_solve(line_field, 2, inverse_y, advection[1], nearby_y)
    line_field = line_solve(line_field, 1, inverse_z, advection[2], nearby_z)
    update = time_step * line_field
    return (update, rms_norm)


def solution(mesh):
    torus = Mesh(
        mesh.devices.reshape(mesh.shape["gx"], 4, 2, mesh.shape["gz"]), ("gx", "gy_0", "gy_1", "gz")
    )
    return jax.shard_map(
        shards,
        mesh=torus,
        in_specs=(P(None, "gz", GY, "gx"), P(), P(), P(), P(), P(), P(), P()),
        out_specs=(P(None, "gz", GY, "gx"), P()),
        check_vma=False,
    )
```

profile of v0, /device:TPU:2, one launch (start us, length us, event | category | flops | bytes accessed | tf_op | source)
XLA Modules:
  0.0 197.9 jit_solution(9758615532742740411)
XLA Ops:
  0.6 3.2 %fusion.83 = (f32[5,32,16,2]{3,2,1,0:T(8,128)}, f32[5,32,16,2]{3,2,1,0:T(8,128)S(1)}) fusion(f32[5,32,16,128]{3,2,1,0:T(8,128)} %param.14), kind=kLoop, calls=%fused_computation.221 | loop fusion | bytes 81920 | tf_op jit(solution)/shard_map/slice | solution.py:24
  3.8 2.6 %copy.124 = f32[5,32,16,2]{1,2,3,0:T(8,128)} copy(f32[5,32,16,2]{3,2,1,0:T(8,128)} %get-tuple-element.46) | data formatting | bytes 40960
  14.2 1.9 collective-permute-start.4
  17.3 4.2 %collective-permute-start.5 = (f32[5,2,16,128]{3,2,1,0:T(8,128)S(1)}, f32[5,2,16,128]{3,2,1,0:T(8,128)}, u32[]{:S(2)}, u32[]{:S(2)}) collective-permute-start(f32[5,2,16,128]{3,2,1,0:T(8,128)S(1)} %get-tuple-element.43), channel_id=1, source_target_pairs={{1,0},{2,1},{3,2},{4,3},{5,4},{6,5},{7,6},{0,7},{9,8},{10,9},{11,1... | collective-permute-start | bytes 245768 | tf_op jit(solution)/shard_map/ppermute | solution.py:28
  23.0 2.5 %copy.85 = f32[5,32,16,2]{3,2,1,0:T(8,128)} copy(f32[5,32,16,2]{1,2,3,0:T(8,128)} %collective-permute-done.1) | data formatting | bytes 40960 | tf_op jit(solution)/shard_map/ppermute | solution.py:28
  25.5 2.4 %pad_maximum_fusion.1 = f32[5,32,16,132]{3,2,1,0:T(8,128)S(1)} fusion(f32[5,32,16,2]{3,2,1,0:T(8,128)} %copy.85, f32[5,32,16,128]{3,2,1,0:T(8,128)S(1)} %copy-done, f32[5,32,16,2]{3,2,1,0:T(8,128)S(1)} %copy.84), kind=kLoop, calls=%fused_computation.5 | loop fusion | flops 675840 | bytes 2703360 | tf_op jit(solution)/shard_map/concatenate | solution.py:34
  35.6 1.9 pad_maximum_fusion
  40.3 9.2 %multiply_reduce_fusion.1 = (f32[5]{0:T(128)S(1)}, f32[5,32,16,128]{3,2,1,0:T(8,128)S(1)}) fusion(f32[5,2,20,132]{3,2,1,0:T(8,128)S(1)} %pad.41, f32[5,32,2,132]{3,2,1,0:T(2,128)S(1)} %pad.39.clone, f32[5,32,16,2]{3,2,1,0:T(8,128)S(1)} %copy-done.1, f32[5,32,16,128]{3,2,1,0:T(8,128)S(1)} %copy-done, f32[5,32,16,2]{3,2,1,0:T(8,128)S(1)} %copy.84, ...), kind=kLoop, calls=%fused_computation.79 | loop fusion | flops 23592956 | bytes 11075860 | tf_op jit(solution)/shard_map/reduce_sum | solution.py:197
  50.8 1.9 fusion.80
  52.7 1.9 copy.96
  54.6 2.5 %copy.97 = f32[5,32,16,2]{1,2,3,0:T(8,128)} copy(f32[5,32,16,2]{3,2,1,0:T(8,128)} %get-tuple-element.41) | data formatting | bytes 40960 | tf_op jit(solution)/shard_map/slice | solution.py:159
  60.9 3.3 %all-to-all-start = ((f32[4,5,4,512]{3,2,1,0:T(4,128)}), f32[4,5,4,512]{3,2,1,0:T(4,128)S(1)}, u32[]{:S(2)}, u32[]{:S(2)}) async-start(f32[4,5,4,512]{3,2,1,0:T(4,128)} %broadcast_in_dim.35), calls=%async_computation | async-start | bytes 327680 | tf_op jit(solution)/shard_map/all_to_all | solution.py:73
  71.5 3.4 %convolution_bitcast_fusion.3 = f32[5,32,16,128]{3,2,1,0:T(8,128)S(1)} fusion(f32[5,32,16,128]{3,2,1,0:T(8,128)S(1)} %fusion.54, f32[5,32,16]{2,1,0:T(8,128)S(1)} %get-tuple-element.71, f32[5,128]{1,0:T(8,128)S(1)} %bitcast.189, f32[5,32,16]{2,1,0:T(8,128)S(1)} %get-tuple-element.70, f32[5,128]{1,0:T(8,128)S(1)} %bitcast.188, ...), kind=kOutput, calls=%fused_computation.14 | convolution fusion | flops 65536000 | bytes 2677760 | tf_op jit(solution)/shard_map/vij,vzjx->vzix/dot_general | solution.py:155
  76.2 2.2 %broadcast_in_dim.38 = f32[8,5,4,4096]{3,2,1,0:T(4,128)} broadcast(f32[5,4,4096]{2,1,0:T(4,128)S(1)} %maximum_bitcast_fusion), dimensions={1,2,3} | broadcast | bytes 2949120 | tf_op jit(solution)/shard_map/broadcast_in_dim | solution.py:74
  78.4 6.2 %all-to-all-start.1 = ((f32[8,5,4,4096]{3,2,1,0:T(4,128)}), f32[8,5,4,4096]{3,2,1,0:T(4,128)}, u32[]{:S(2)}, u32[]{:S(2)}) async-start(f32[8,5,4,4096]{3,2,1,0:T(4,128)} %broadcast_in_dim.38), calls=%async_computation.1 | async-start | bytes 5242880 | tf_op jit(solution)/shard_map/all_to_all | solution.py:73
  86.9 29.1 %all-to-all-done.1 = f32[8,5,4,4096]{3,2,1,0:T(4,128)} async-done(((f32[8,5,4,4096]{3,2,1,0:T(4,128)}), f32[8,5,4,4096]{3,2,1,0:T(4,128)}, u32[]{:S(2)}, u32[]{:S(2)}) %all-to-all-start.1) | async-done | bytes 2621472 | tf_op jit(solution)/shard_map/all_to_all | solution.py:73
  116.0 3.6 %copy.106 = f32[5,8,4,4096]{3,2,1,0:T(4,128)} copy(f32[5,8,4,4096]{3,2,0,1:T(4,128)} %bitcast.46) | data formatting | bytes 5242880 | tf_op jit(solution)/shard_map/transpose | solution.py:66
  119.6 4.0 %reshape.550 = f32[5,32,4096]{2,1,0:T(8,128)} reshape(f32[5,8,4,4096]{3,2,1,0:T(4,128)} %copy.106) | data formatting | bytes 5242880 | tf_op jit(solution)/shard_map/reshape | solution.py:68
  123.6 3.2 %convolution_bitcast_fusion = f32[4,5,4096]{2,0,1:T(4,128)S(1)} fusion(f32[5,32,4096]{2,1,0:T(8,128)} %reshape.550, f32[4,5,32]{2,1,0:T(8,128)S(1)} %constant_dynamic-slice_fusion.1), kind=kOutput, calls=%fused_computation.3 | convolution fusion | flops 31457280 | bytes 2951680 | tf_op jit(solution)/shard_map/rvq,vqn->rvn/dot_general | solution.py:145
  131.9 6.0 %all-to-all-start.2 = ((f32[8,5,4,2048]{3,2,1,0:T(4,128)}), f32[8,5,4,2048]{3,2,1,0:T(4,128)S(1)}, u32[]{:S(2)}, u32[]{:S(2)}) async-start(f32[8,5,4,2048]{3,2,1,0:T(4,128)} %broadcast_in_dim.41), calls=%async_computation.2 | async-start | bytes 2621440 | tf_op jit(solution)/shard_map/all_to_all | solution.py:73
  139.6 10.2 %all-gather.4 = f32[4,2,5]{2,1,0:T(2,128)S(1)} all-gather(f32[1,2,5]{2,1,0:T(2,128)S(1)} %maximum_bitcast_fusion.3), channel_id=2, replica_groups=mesh['gx'=4,'gy_0'=4,'gy_1'=2,'gz'=8] {'gx'}, dimensions={0}, use_global_device_ids=true | all-gather | bytes 200 | tf_op jit(solution)/shard_map/all_gather | solution.py:47
  153.0 8.4 %all-gather.5 = f32[4,2,5]{2,1,0:T(2,128)S(1)} all-gather(f32[1,2,5]{2,1,0:T(2,128)S(1)} %maximum_bitcast_fusion.4), channel_id=3, replica_groups=mesh['gx'=4,'gy_0'=4,'gy_1'=2,'gz'=8] {'gy_0'}, dimensions={0}, use_global_device_ids=true | all-gather | bytes 200 | tf_op jit(solution)/shard_map/all_gather | solution.py:47
  164.8 1.8 all-gather.6
  168.5 16.5 %all-gather.7 = f32[8,2,5]{2,1,0:T(2,128)S(1)} all-gather(f32[1,2,5]{2,1,0:T(2,128)S(1)} %maximum_bitcast_fusion.6), channel_id=5, replica_groups=mesh['gx'=4,'gy_0'=4,'gy_1'=2,'gz'=8] {'gz'}, dimensions={0}, use_global_device_ids=true | all-gather | bytes 360 | tf_op jit(solution)/shard_map/all_gather | solution.py:47
  (151 shorter events, 52.7 us)
Async XLA Ops:
  3.8 7.1 %copy-start = (f32[5,32,16,128]{3,2,1,0:T(8,128)S(1)}, f32[5,32,16,128]{3,2,1,0:T(8,128)}, u32[]{:S(2)}) copy-start(f32[5,32,16,128]{3,2,1,0:T(8,128)} %param.14) | copy-start | bytes 3932164
  6.5 10.8 %collective-permute-start = (f32[5,32,16,2]{1,2,3,0:T(8,128)}, f32[5,32,16,2]{1,2,3,0:T(8,128)}, u32[]{:S(2)}, u32[]{:S(2)}) collective-permute-start(f32[5,32,16,2]{1,2,3,0:T(8,128)} %copy.124), channel_id=1, source_target_pairs={{0,64},{64,128},{128,192},{192,0},{1,65},{65,129},{129,193},{193,1... | collective-permute-start | bytes 61448 | tf_op jit(solution)/shard_map/ppermute | solution.py:27
  8.0 8.0 %copy-start.2 = (f32[5,128,128]{2,1,0:T(8,128)S(1)}, f32[5,128,128]{2,1,0:T(8,128)}, u32[]{:S(2)}) copy-start(f32[5,128,128]{2,1,0:T(8,128)} %param.16) | copy-start | bytes 983044
  9.3 13.7 %collective-permute-start.1 = (f32[5,32,16,2]{1,2,3,0:T(8,128)}, f32[5,32,16,2]{1,2,3,0:T(8,128)}, u32[]{:S(2)}, u32[]{:S(2)}) collective-permute-start(f32[5,32,16,2]{1,2,3,0:T(8,128)} %copy.125), channel_id=1, source_target_pairs={{64,0},{128,64},{192,128},{0,192},{65,1},{129,65},{193,129},{1,193... | collective-permute-start | bytes 61448 | tf_op jit(solution)/shard_map/ppermute | solution.py:28
  11.7 20.5 %collective-permute-start.2 = (f32[5,32,2,128]{3,1,2,0:T(8,128)}, f32[5,32,2,128]{3,1,2,0:T(8,128)}, u32[]{:S(2)}, u32[]{:S(2)}) collective-permute-start(f32[5,32,2,128]{3,1,2,0:T(8,128)} %copy.126), channel_id=1, source_target_pairs={{0,8},{8,16},{16,24},{24,32},{32,40},{40,48},{48,56},{56,0},{1,9},... | collective-permute-start | bytes 491528 | tf_op jit(solution)/shard_map/ppermute | solution.py:27
  11.8 21.9 %collective-permute-start.3 = (f32[5,32,2,128]{3,1,2,0:T(8,128)S(1)}, f32[5,32,2,128]{3,1,2,0:T(8,128)}, u32[]{:S(2)}, u32[]{:S(2)}) collective-permute-start(f32[5,32,2,128]{3,1,2,0:T(8,128)S(1)} %copy.127), channel_id=1, source_target_pairs={{8,0},{16,8},{24,16},{32,24},{40,32},{48,40},{56,48},{0,56},{9,1},... | collective-permute-start | bytes 491528 | tf_op jit(solution)/shard_map/ppermute | solution.py:28
  14.2 3.1 %copy-start.10 = (f32[3,5]{1,0:T(4,128)S(1)}, f32[3,5]{1,0:T(4,128)}, u32[]{:S(2)}) copy-start(f32[3,5]{1,0:T(4,128)} %param.15) | copy-start | bytes 184
  14.2 15.9 %collective-permute-start.4 = (f32[5,2,16,128]{3,2,1,0:T(8,128)}, f32[5,2,16,128]{3,2,1,0:T(8,128)}, u32[]{:S(2)}, u32[]{:S(2)}) collective-permute-start(f32[5,2,16,128]{3,2,1,0:T(8,128)} %get-tuple-element.42), channel_id=1, source_target_pairs={{0,1},{1,2},{2,3},{3,4},{4,5},{5,6},{6,7},{7,0},{8,9},{9,10},{10,1... | collective-permute-start | bytes 245768 | tf_op jit(solution)/shard_map/ppermute | solution.py:27
  17.3 13.9 %collective-permute-start.5 = (f32[5,2,16,128]{3,2,1,0:T(8,128)S(1)}, f32[5,2,16,128]{3,2,1,0:T(8,128)}, u32[]{:S(2)}, u32[]{:S(2)}) collective-permute-start(f32[5,2,16,128]{3,2,1,0:T(8,128)S(1)} %get-tuple-element.43), channel_id=1, source_target_pairs={{1,0},{2,1},{3,2},{4,3},{5,4},{6,5},{7,6},{0,7},{9,8},{10,9},{11,1... | collective-permute-start | bytes 245768 | tf_op jit(solution)/shard_map/ppermute | solution.py:28
  30.1 5.1 %copy-start.1 = (f32[5,32,16,2]{3,2,1,0:T(8,128)S(1)}, f32[5,32,16,2]{3,2,1,0:T(8,128)}, u32[]{:S(2)}) copy-start(f32[5,32,16,2]{3,2,1,0:T(8,128)} %copy.85) | copy-start | bytes 61444
  54.6 9.6 %copy-start.11 = (s32[16]{0:T(128)S(1)}, s32[16]{0:T(128)}, u32[]{:S(2)}) copy-start(s32[16]{0:T(128)} %constant.116) | copy-start | bytes 196
  57.2 11.5 %copy-start.6 = (f32[5,128,1]{2,1,0:T(8,128)S(1)}, f32[5,128,1]{2,1,0:T(8,128)}, u32[]{:S(2)}) copy-start(f32[5,128,1]{2,1,0:T(8,128)} %get-tuple-element.53) | copy-start | bytes 7684
  60.9 9.7 %all-to-all-start = ((f32[4,5,4,512]{3,2,1,0:T(4,128)}), f32[4,5,4,512]{3,2,1,0:T(4,128)S(1)}, u32[]{:S(2)}, u32[]{:S(2)}) async-start(f32[4,5,4,512]{3,2,1,0:T(4,128)} %broadcast_in_dim.35), calls=%async_computation | async-start | bytes 327680 | tf_op jit(solution)/shard_map/all_to_all | solution.py:73
  68.8 2.6 %copy-start.7 = (f32[5,16,16]{2,1,0:T(8,128)S(1)}, f32[5,16,16]{2,1,0:T(8,128)}, u32[]{:S(2)}) copy-start(f32[5,16,16]{2,1,0:T(8,128)} %param.17) | copy-start | bytes 15364
  74.9 1.1 copy-start.3
  78.4 6.2 %copy-start.8 = (f32[5,32,32]{2,1,0:T(8,128)S(1)}, f32[5,32,32]{2,1,0:T(8,128)}, u32[]{:S(2)}) copy-start(f32[5,32,32]{2,1,0:T(8,128)} %param.20) | copy-start | bytes 61444
  78.4 37.6 %all-to-all-start.1 = ((f32[8,5,4,4096]{3,2,1,0:T(4,128)}), f32[8,5,4,4096]{3,2,1,0:T(4,128)}, u32[]{:S(2)}, u32[]{:S(2)}) async-start(f32[8,5,4,4096]{3,2,1,0:T(4,128)} %broadcast_in_dim.38), calls=%async_computation.1 | async-start | bytes 5242880 | tf_op jit(solution)/shard_map/all_to_all | solution.py:73
  85.8 0.9 copy-start.5
  126.8 1.3 copy-start.4
  131.9 6.6 %copy-start.9 = (f32[5,32,32]{2,1,0:T(8,128)S(1)}, f32[5,32,32]{2,1,0:T(8,128)}, u32[]{:S(2)}) copy-start(f32[5,32,32]{2,1,0:T(8,128)} %param.21) | copy-start | bytes 61444
  131.9 59.6 %all-to-all-start.2 = ((f32[8,5,4,2048]{3,2,1,0:T(4,128)}), f32[8,5,4,2048]{3,2,1,0:T(4,128)S(1)}, u32[]{:S(2)}, u32[]{:S(2)}) async-start(f32[8,5,4,2048]{3,2,1,0:T(4,128)} %broadcast_in_dim.41), calls=%async_computation.2 | async-start | bytes 2621440 | tf_op jit(solution)/shard_map/all_to_all | solution.py:73
where the time goes:
time: 199 us; the launch traced here: 198 us
  local copies, waits for them, and re-layouts  57.7 us (29%)
  blocking collectives  37 us (19%)
  waiting for transfers between devices  29.1 us (15%)
  starting transfers between devices  26.6 us (13%)
  other arithmetic  24 us (12%)
  between operations  13 us (7%)
  matrix products  10.5 us (5%)
    all_gather x4, blocking collectives, collected_together(): both, at, found = (lax.all_gather(jnp.concatenate(lines), axis), 0, {})  37 us
    all_to_all x3, waiting for transfers between devices, from_everyone(): lax.all_to_all(jnp.broadcast_to(shard[None], (devices, *shard.shape)), ax...  29.1 us
    all_to_all x3, starting transfers between devices, from_everyone(): lax.all_to_all(jnp.broadcast_to(shard[None], (devices, *shard.shape)), ax...  15.5 us
    unnamed x46, local copies, waits for them, and re-layouts  14.9 us
    reduce_sum x1, other arithmetic, shards(): local_sums = jnp.sum(residual * residual, axis=(1, 2, 3))  9.21 us
    ppermute x3, starting transfers between devices, padded_2(): lax.ppermute(first, axis, [(b, a) for a, b in up])  7.61 us
    dot_general x3, matrix products, line_solve(): jnp.einsum(patterns[line_axis], inverse, line_field, precision=exact_mode)  6.31 us
    reshape x3, local copies, waits for them, and re-layouts, in_order(): parts.reshape(*dims[:dim], dims[dim] * dims[dim + 1], *dims[dim + 2:])  5.79 us
  transfers between devices with their start and end apart: 9, of which 1 were waited for; matrix products, arithmetic and copies ran while one was open for 15% of the time, Pallas kernels for 0%

commit v1 on v0

v1 whole, which is shorter than its diff:
```python
import functools

import jax
import jax.numpy as jnp
from jax import lax
from jax.experimental import pallas as pl
from jax.experimental.pallas import tpu as pltpu
from jax.sharding import PartitionSpec as P

VARS = 5
F32 = jnp.float32
BF16 = jnp.bfloat16
DAMP = 0.0625
COURANT = 8000.0
VMEM = pltpu.VMEM
NN = (((1,), (0,)), ((), ()))
NT = (((1,), (1,)), ((), ()))


def iota(shape, dim):
    return lax.broadcasted_iota(jnp.int32, shape, dim)


def picks(shape, cond):
    return jnp.where(cond(iota(shape, 0), iota(shape, 1)), 1.0, 0.0).astype(BF16)


def split(x):
    hi = x.astype(BF16)
    return hi, (x - hi.astype(F32)).astype(BF16)


def dot1(a, b, dims=NN):
    return lax.dot_general(a, b, dims, preferred_element_type=F32)


def dot3(a, b, dims=NN):
    return dot1(a[0], b[0], dims) + (dot1(a[0], b[1], dims) + dot1(a[1], b[0], dims))


def call(body, out, args, scratch=(), smem=0, flops=1_000_000):
    specs = [pl.BlockSpec(memory_space=pltpu.SMEM)] * smem
    specs += [pl.BlockSpec(memory_space=VMEM)] * (len(args) - smem)
    size = sum(a.size * a.dtype.itemsize for a in args)
    return pl.pallas_call(
        body,
        out_shape=[jax.ShapeDtypeStruct(*o) for o in out],
        in_specs=specs,
        out_specs=[pl.BlockSpec(memory_space=VMEM)] * len(out),
        scratch_shapes=[VMEM(*s) for s in scratch],
        compiler_params=pltpu.CompilerParams(vmem_limit_bytes=36 * 1024 * 1024),
        cost_estimate=pl.CostEstimate(flops=flops, bytes_accessed=size, transcendentals=0),
    )(*args)


def tables_body(adv, idx, invx, invy, invz, redx, redy, redz, ax, qx, ay, qy, az, qz, qzy, nx, my, mz):
    ix = idx[0]
    nx[...] = jnp.zeros_like(nx)

    def spread(left, parts, right, keep, write):
        for k, part in enumerate(parts):
            wide = dot1(dot1(left, part).astype(BF16), right)
            write(k, (jnp.where(keep, wide, 0.0) if keep is not None else wide).astype(BF16))

    def masked(shape, cond):
        return cond(iota(shape, 0), iota(shape, 1))

    def near(red, speed):
        rows = red.shape[0]
        i, k = iota((rows, rows), 0), iota((rows, rows), 1)
        r, d = i & 3, k - (i - (i & 3))
        lower, upper = -0.5 * speed - 2.0, 0.5 * speed - 2.0
        half = jnp.where(
            ((r == 0) & (d == -2)) | ((r == 1) & (d == -1)) | ((r == 2) & (d == 4)) | ((r == 3) & (d == 5)),
            0.5,
            0.0,
        )
        other = jnp.where((r == 0) & (d == -1), lower, jnp.where((r == 3) & (d == 4), upper, 0.0))
        return lax.dot_general(half + other, red, NN, precision=lax.Precision.HIGHEST, preferred_element_type=F32)

    def per_variable(v, carry):
        parts = split(invx[v])
        pick = picks((128, 128), lambda a, c: ((a >> 2) == v) & (c == ((126 + (a & 3)) & 127)))
        for k in range(2):
            ax[2 * v + k] = parts[k]
            qx[2 * v + k] = dot1(pick, parts[k], NT).astype(BF16)

        def put(ref):
            def write(k, value):
                ref[2 * v + k] = value

            return write

        parts = split(invy[v])
        spread(
            picks((128, 16), lambda a, k: (a & 15) == k),
            parts,
            picks((16, 128), lambda k, c: k == (c & 15)),
            masked((128, 128), lambda a, c: (a >> 4) == (c >> 4)),
            put(ay),
        )
        spread(
            picks((512, 16), lambda a, k: (a & 15) == k),
            parts,
            picks((16, 128), lambda k, c: k == (c & 3) + 12 * ((c & 3) >> 1)),
            masked((512, 128), lambda a, c: (((a >> 4) & 7) == (c >> 4)) & ((a >> 7) == ((c >> 2) & 3))),
            put(qy),
        )
        parts = split(invz[v])
        left = picks((256, 32), lambda a, k: (a >> 3) == k)
        spread(
            left,
            parts,
            picks((32, 256), lambda k, c: k == (c >> 3)),
            masked((256, 256), lambda a, c: (a & 7) == (c & 7)),
            put(az),
        )
        spread(
            left,
            parts,
            picks((32, 32), lambda k, c: k == (c >> 3) + 28 * (c >> 4)),
            masked((256, 32), lambda a, c: (a & 7) == (c & 7)),
            put(qz),
        )
        spread(
            picks((128, 32), lambda a, k: k == ((a >> 2) & 3) * 8 + (a >> 4)),
            parts,
            picks((32, 16), lambda k, c: k == (c >> 2) + 28 * (c >> 3)),
            masked((128, 16), lambda a, c: (a & 3) == (c & 3)),
            put(qzy),
        )
        parts = split(near(redy[v], adv[1, v]))
        spread(
            picks((128, 32), lambda a, k: k == 4 * (a >> 4) + (a & 3)),
            parts,
            picks((32, 128), lambda k, c: k == 4 * (c >> 4) + (c & 3)),
            masked((128, 128), lambda a, c: ((a >> 2) & 3) == ((c >> 2) & 3)),
            put(my),
        )
        parts = split(near(redz[v], adv[2, v]))
        spread(
            picks((64, 32), lambda a, k: k == 4 * (a >> 3) + (a & 3)),
            parts,
            picks((32, 64), lambda k, c: k == 4 * (c >> 3) + (c & 3)),
            masked((64, 64), lambda a, c: ((a >> 2) & 1) == ((c >> 2) & 1)),
            put(mz),
        )
        parts = split(near(redx[v], adv[0, v]))
        left = picks((32, 16), lambda a, k: ((a >> 2) == v) & (k == 4 * ix + ((a & 3) ^ 2)))
        for s in range(4):
            peer = (ix + 4 - s) & 3

            def add(k, value, s=s):
                nx[2 * s + k] += value

            spread(
                left,
                parts,
                picks((16, 32), lambda k, c: ((c >> 2) == v) & (k == 4 * peer + ((c & 3) ^ 2))),
                None,
                add,
            )
        return carry

    lax.fori_loop(0, VARS, per_variable, 0)


def tables(idx, advection, *small):
    shapes = [
        (10, 128, 128),
        (10, 128, 128),
        (10, 128, 128),
        (10, 512, 128),
        (10, 256, 256),
        (10, 256, 32),
        (10, 128, 16),
        (8, 32, 32),
        (10, 128, 128),
        (10, 64, 64),
    ]
    return call(
        tables_body, [(s, BF16) for s in shapes], (advection, idx, *small), smem=2, flops=20_000_000
    )


def faces_body(u, xlo, xhi, ylo, yhi, zlo, zhi):
    lane = iota((512, 128), 1)
    wide = jnp.zeros((512, 128), F32)
    for v in range(VARS):
        block = u[512 * v : 512 * v + 512, :]
        low = pltpu.roll(block, 2 * v, 1) if v else block
        wide = jnp.where((lane >> 1) == v, low, wide)
        wide = jnp.where((lane >> 1) == 8 + v, pltpu.roll(block, 18 + 2 * v, 1), wide)
        for j in range(2):
            at = 32 * (2 * v + j)
            ylo[at : at + 32, :] = u[pl.ds(512 * v + j, 32, stride=16), :]
            yhi[at : at + 32, :] = u[pl.ds(512 * v + 14 + j, 32, stride=16), :]
        zlo[32 * v : 32 * v + 32, :] = u[512 * v : 512 * v + 32, :]
        zhi[32 * v : 32 * v + 32, :] = u[512 * v + 480 : 512 * v + 512, :]
    turned = wide.T
    xlo[...] = turned[0:16]
    xhi[...] = turned[16:32]


def primitives(u):
    inverse = 1.0 / u[0]
    velocity = [u[1 + k] * inverse for k in range(3)]
    kinetic = 0.5 * (velocity[0] * velocity[0] + velocity[1] * velocity[1] + velocity[2] * velocity[2])
    internal = jnp.maximum(u[4] * inverse - kinetic, 0.25)
    return velocity, internal, 0.4 * u[0] * internal


def flux(u, velocity, pressure, d):
    w = velocity[d]
    out = [u[1 + d]]
    for k in range(3):
        moment = u[1 + k] * w
        out.append(moment + pressure if k == d else moment)
    out.append((u[4] + pressure) * w)
    return out


def stats_row(shape, sums, top):
    lane = iota(shape, len(shape) - 1)
    row = jnp.where(lane == VARS, top, 0.0)
    for v in range(VARS):
        row = jnp.where(lane == v, sums[v], row)
    return row


def merged_stats(rows):
    lane = iota(rows[0].shape, 1)
    total, top = rows[0], rows[0]
    for row in rows[1:]:
        total, top = total + row, jnp.maximum(top, row)
    return jnp.where(lane < VARS, total, top)


def residual_body(
    u, xlo, xhi, ylo, yhi, zlo, zhi, own_lo, own_hi, ax, ay, az, w, bx, pad, fy, fz, res, fix, half, edge
):
    def fill(z, carry):
        for v in range(VARS):
            pad[36 * v + 2 + z, 8:24, :] = u[pl.ds(pl.multiple_of(512 * v + 16 * z, 16), 16), :]
        return carry

    lax.fori_loop(0, 32, fill, 0)
    rows = pad.reshape(180 * 32, 128)
    for v in range(VARS):
        for k in range(2):
            pad[36 * v + k, 8:24, :] = zlo[32 * v + 16 * k : 32 * v + 16 * k + 16, :]
            pad[36 * v + 34 + k, 8:24, :] = zhi[32 * v + 16 * k : 32 * v + 16 * k + 16, :]
            at = 32 * (2 * v + k)
            rows[pl.ds(32 * (36 * v + 2) + 6 + k, 32, stride=32), :] = ylo[at : at + 32, :]
            rows[pl.ds(32 * (36 * v + 2) + 24 + k, 32, stride=32), :] = yhi[at : at + 32, :]

    edge[...] = jnp.zeros_like(edge)

    def line(ref, j):
        return [ref[2 * v + j : 2 * v + j + 1, :] for v in range(VARS)]

    def fx(u):
        velocity, _, pressure = primitives(u)
        return flux(u, velocity, pressure, 0)

    l2, l1, h1, h2 = line(xlo, 0), line(xlo, 1), line(xhi, 0), line(xhi, 1)
    o0, o1, p1, p0 = line(own_lo, 0), line(own_lo, 1), line(own_hi, 0), line(own_hi, 1)
    fl, fp, fh, fo = fx(l1), fx(p0), fx(h1), fx(o0)
    for v in range(VARS):
        dl, dh = l1[v] - p0[v], h1[v] - o0[v]
        edge[4 * v : 4 * v + 1, :] = -DAMP * dh
        edge[4 * v + 1 : 4 * v + 2, :] = -0.5 * (fh[v] - fo[v]) + 4.0 * DAMP * dh - DAMP * (h2[v] - o1[v])
        edge[4 * v + 2 : 4 * v + 3, :] = 0.5 * (fl[v] - fp[v]) + 4.0 * DAMP * dl - DAMP * (l2[v] - p1[v])
        edge[4 * v + 3 : 4 * v + 4, :] = -DAMP * dl
    fix[...] = edge[...].T

    for z in (-1, 32):
        c = [pad[36 * v + 2 + z, 8:24, :] for v in range(VARS)]
        velocity, _, pressure = primitives(c)
        for v, f in enumerate(flux(c, velocity, pressure, 2)):
            fz[34 * v + 1 + z] = f

    def plane(z, top):
        full = [pad[36 * v + 2 + z] for v in range(VARS)]
        velocity, internal, pressure = primitives(full)
        for v, f in enumerate(flux(full, velocity, pressure, 1)):
            fy[32 * v + z] = f
        c = [f[8:24] for f in full]
        velocity, internal, pressure = [f[8:24] for f in velocity], internal[8:24], pressure[8:24]
        for v, f in enumerate(flux(c, velocity, pressure, 2)):
            fz[34 * v + 1 + z] = f
        for v, f in enumerate(flux(c, velocity, pressure, 0)):
            damped = (4.0 * DAMP) * c[v]
            res[32 * v + z] = (
                pltpu.roll(damped - 0.5 * f, 127, 1)
                + pltpu.roll(damped + 0.5 * f, 1, 1)
                - DAMP * (pltpu.roll(c[v], 126, 1) + pltpu.roll(c[v], 2, 1))
                - (18.0 * DAMP) * c[v]
            )
        speed = jnp.abs(velocity[0]) + jnp.abs(velocity[1]) + jnp.abs(velocity[2])
        return jnp.maximum(top, speed + jnp.sqrt((3.0 * 1.4 * 0.4) * internal))

    top = lax.fori_loop(0, 32, plane, jnp.zeros((16, 128), F32))

    lane = iota((16, 128), 1)
    edges = (lane < 2) | (lane >= 126)

    def finish(z, sums):
        out = []
        fixes = fix[pl.ds(pl.multiple_of(16 * z, 16), 16), :]
        for v in range(VARS):
            at = 36 * v + 2 + z
            ones = (pad[at, 7:23, :] + pad[at, 9:25, :]) + (pad[at - 1, 8:24, :] + pad[at + 1, 8:24, :])
            twos = (pad[at, 6:22, :] + pad[at, 10:26, :]) + (pad[at - 2, 8:24, :] + pad[at + 2, 8:24, :])
            steep = (fy[32 * v + z, 7:23, :] - fy[32 * v + z, 9:25, :]) + (fz[34 * v + z] - fz[34 * v + 2 + z])
            value = res[32 * v + z] + 0.5 * steep + (4.0 * DAMP) * ones - DAMP * twos
            value = value + jnp.where(edges, pltpu.roll(fixes, (126 - 4 * v) & 127, 1), 0.0)
            res[32 * v + z] = value
            out.append(sums[v] + value * value)
        return tuple(out)

    sums = lax.fori_loop(0, 32, finish, tuple(jnp.zeros((16, 128), F32) for _ in range(VARS)))

    def solve(v, carry):
        field = res[pl.ds(32 * v, 32)].reshape(512, 128)
        half[...] = dot3(split(field), (ax[2 * v], ax[2 * v + 1]), NT)
        table = (ay[2 * v], ay[2 * v + 1])
        for g in range(4):
            half[128 * g : 128 * g + 128, :] = dot3(table, split(half[128 * g : 128 * g + 128, :]))
        table = (az[2 * v], az[2 * v + 1])
        field = half[...].reshape(32, 2, 8, 128)
        parts = [dot3(table, split(field[:, h].reshape(256, 128))).reshape(32, 1, 8, 128) for h in range(2)]
        w[pl.ds(pl.multiple_of(512 * v, 512), 512), :] = jnp.concatenate(parts, axis=1).reshape(512, 128)
        return carry

    lax.fori_loop(0, VARS, solve, 0)
    lane = iota((512, 128), 1)
    wide = jnp.zeros((512, 128), F32)
    for v in range(VARS):
        wide = jnp.where((lane >> 2) == v, pltpu.roll(w[512 * v : 512 * v + 512, :], 2 + 4 * v, 1), wide)
    turned = wide.T
    bx[...] = turned[0:24]
    bx[20:21, :] = stats_row((1, 512), [jnp.sum(s) for s in sums], jnp.max(top))


def spread_body(w, b0, b1, b2, b3, nx, qx, v1, yp, zp, wide, yb, zb):
    total = None
    blank = jnp.zeros((8, 512), F32)
    pieces = [b0, b1, b2, b3]
    for s in range(4):
        term = dot3((nx[2 * s], nx[2 * s + 1]), split(jnp.concatenate([pieces[s][...], blank], axis=0)))
        total = term if total is None else total + term
    wide[...] = jnp.zeros_like(wide)
    wide[0:32, :] = total
    turned = split(wide[...].T)

    def correct(v, carry):
        at = pl.ds(pl.multiple_of(512 * v, 512), 512)
        v1[at, :] = w[at, :] - dot3(turned, (qx[2 * v], qx[2 * v + 1]))
        return carry

    lax.fori_loop(0, VARS, correct, 0)
    for v in range(VARS):
        for t in range(4):
            for j, y in enumerate((0, 1, 14, 15)):
                at = ((v * 4 + t) * 4 + j) * 8
                yb[at : at + 8, :] = v1[pl.ds(512 * v + 128 * t + y, 8, stride=16), :]
        for h in range(2):
            for j, z in enumerate((0, 1, 30, 31)):
                at = ((v * 2 + h) * 4 + j) * 8
                zb[at : at + 8, :] = v1[512 * v + 16 * z + 8 * h : 512 * v + 16 * z + 8 * h + 8, :]
    stats = merged_stats([p[20:21, 0:128] for p in pieces])
    for p in range(8):
        yp[88 * p : 88 * p + 80, :] = yb[pl.ds(p, 80, stride=8), :]
        yp[88 * p + 80 : 88 * p + 88, :] = jnp.broadcast_to(stats, (8, 128))
        zp[40 * p : 40 * p + 40, :] = zb[pl.ds(p, 40, stride=8), :]


def owner_y_body(yr, my, yo, st):
    def one(v, carry):
        at = pl.multiple_of(16 * v, 16)
        data = jnp.concatenate([yr[pl.ds(88 * q + at, 16), :] for q in range(8)], axis=0)
        out = dot3((my[2 * v], my[2 * v + 1]), split(data))
        for p in range(8):
            yo[pl.ds(80 * p + at, 16), :] = out[16 * p : 16 * p + 16]
        return carry

    lax.fori_loop(0, VARS, one, 0)
    st[...] = merged_stats([yr[88 * q + 80 : 88 * q + 88, :] for q in range(8)])


def owner_z_body(zr, st, mz, zo):
    def one(v, carry):
        at = pl.multiple_of(8 * v, 8)
        data = jnp.concatenate([zr[pl.ds(40 * q + at, 8), :] for q in range(8)], axis=0)
        out = dot3((mz[2 * v], mz[2 * v + 1]), split(data))
        for p in range(8):
            zo[pl.ds(48 * p + at, 8), :] = out[8 * p : 8 * p + 8]
        return carry

    lax.fori_loop(0, VARS, one, 0)
    for p in range(8):
        zo[48 * p + 40 : 48 * p + 48, :] = st[...]


def cross_body(zg, zc, zy, fin):
    for v in range(VARS):
        for h in range(2):
            for r in range(4):
                at = ((v * 2 + h) * 4 + r) * 8
                zc[at : at + 8, :] = zg[pl.ds(8 * v + 4 * h + r, 8, stride=48), :]
        for j, (c, h) in enumerate(((0, 0), (1, 0), (6, 1), (7, 1))):
            zy[pl.ds(16 * v + j, 4, stride=4), :] = zg[48 * c + 8 * v + 4 * h : 48 * c + 8 * v + 4 * h + 4, :]
    for p in range(1, 8):
        zy[80 * p : 80 * p + 80, :] = zy[0:80, :]
    stats = merged_stats([zg[48 * q + 40 : 48 * q + 48, :] for q in range(8)])
    lane = iota((8, 128), 1)
    top = jnp.max(jnp.where(lane == VARS, stats, 0.0))
    norm = jnp.sqrt(stats * (1.0 / 16777216.0))
    fin[...] = jnp.where(lane == VARS, COURANT / top, norm)


def middle_body(v1, zc, yg, qz, qy, v2):
    def one(v, carry):
        base = pl.multiple_of(512 * v, 512)
        at = pl.multiple_of(16 * v, 16)
        data = jnp.concatenate([yg[pl.ds(80 * c + at, 16), :] for c in range(8)], axis=0)
        v2[pl.ds(base, 512), :] = v1[pl.ds(base, 512), :] - dot3((qy[2 * v], qy[2 * v + 1]), split(data))
        table = (qz[2 * v], qz[2 * v + 1])
        parts = []
        for h in range(2):
            rows = zc[pl.ds(pl.multiple_of(64 * v + 32 * h, 32), 32), :]
            parts.append(dot3(table, split(rows)).reshape(32, 1, 8, 128))
        v2[pl.ds(base, 512), :] -= jnp.concatenate(parts, axis=1).reshape(512, 128)
        return carry

    lax.fori_loop(0, VARS, one, 0)


def last_body(idx, v2, zr, fin, my, qzy, qy, out):
    iy = idx[1]
    lane = iota((8, 128), 1)
    step = jnp.max(jnp.where(lane == VARS, fin[...], 0.0))

    def one(v, carry):
        base = pl.multiple_of(512 * v, 512)
        at = pl.multiple_of(16 * v, 16)
        data = jnp.concatenate([zr[pl.ds(80 * q + at, 16), :] for q in range(8)], axis=0)
        mine = pl.ds(pl.multiple_of(16 * iy, 16), 16)
        crossed = dot3((my[2 * v, mine, :], my[2 * v + 1, mine, :]), split(data))
        lines = dot3((qzy[2 * v], qzy[2 * v + 1]), split(crossed))
        value = v2[pl.ds(base, 512), :] + dot3((qy[2 * v], qy[2 * v + 1]), split(lines))
        out[pl.ds(base, 512), :] = step * value
        return carry

    lax.fori_loop(0, VARS, one, 0)


def handed(x, axis):
    return lax.all_to_all(x, axis, 0, 0, tiled=True)


def shifted(x, axis, by):
    size = lax.axis_size(axis)
    return lax.ppermute(x, axis, [(i, (i + by) % size) for i in range(size)])


def shards(flow_state, advection, inverse_x, inverse_y, inverse_z, reduced_x, reduced_y, reduced_z):
    idx = jnp.stack([lax.axis_index(a) for a in ("gx", "gy", "gz")]).astype(jnp.int32)
    u = flow_state.reshape(2560, 128)
    xlo, xhi, ylo, yhi, zlo, zhi = call(
        faces_body,
        [((16, 512), F32), ((16, 512), F32), ((320, 128), F32), ((320, 128), F32), ((160, 128), F32), ((160, 128), F32)],
        (u,),
    )
    from_zlo, from_zhi = shifted(zhi, "gz", 1), shifted(zlo, "gz", -1)
    from_ylo, from_yhi = shifted(yhi, "gy", 1), shifted(ylo, "gy", -1)
    from_xlo, from_xhi = shifted(xhi, "gx", 1), shifted(xlo, "gx", -1)
    ax, qx, ay, qy, az, qz, qzy, nx, my, mz = tables(
        idx, advection, inverse_x, inverse_y, inverse_z, reduced_x, reduced_y, reduced_z
    )
    w, bx = call(
        residual_body,
        [((2560, 128), F32), ((24, 512), F32)],
        (u, from_xlo, from_xhi, from_ylo, from_yhi, from_zlo, from_zhi, xlo, xhi, ax, ay, az),
        scratch=[
            ((180, 32, 128), F32),
            ((160, 32, 128), F32),
            ((170, 16, 128), F32),
            ((160, 16, 128), F32),
            ((512, 128), F32),
            ((512, 128), F32),
            ((128, 512), F32),
        ],
    )
    v1, yp, zp = call(
        spread_body,
        [((2560, 128), F32), ((704, 128), F32), ((320, 128), F32)],
        (w, bx, shifted(bx, "gx", 1), shifted(bx, "gx", 2), shifted(bx, "gx", 3), nx, qx),
        scratch=[((128, 512), F32), ((640, 128), F32), ((320, 128), F32)],
    )
    yr, zr = handed(yp, "gy"), handed(zp, "gz")
    yo, st = call(owner_y_body, [((640, 128), F32), ((8, 128), F32)], (yr, my))
    yg = handed(yo, "gy")
    (zo,) = call(owner_z_body, [((384, 128), F32)], (zr, st, mz))
    zg = handed(zo, "gz")
    zc, zy, fin = call(cross_body, [((320, 128), F32), ((640, 128), F32), ((8, 128), F32)], (zg,))
    zyg = handed(zy, "gy")
    (v2,) = call(middle_body, [((2560, 128), F32)], (v1, zc, yg, qz, qy))
    (out,) = call(last_body, [((2560, 128), F32)], (idx, v2, zyg, fin, my, qzy, qy), smem=1)
    return out.reshape(5, 32, 16, 128), fin[0, :VARS]


def solution(mesh):
    spec = P(None, "gz", "gy", "gx")
    return jax.shard_map(
        shards,
        mesh=mesh,
        in_specs=(spec, P(), P(), P(), P(), P(), P(), P()),
        out_specs=(spec, P()),
        check_vma=False,
    )
```

time: 199 us -> 127 us (0.64)
  local copies, waits for them, and re-layouts: 57.7 us -> 16.1 us
  Pallas kernels: 0 us -> 34.3 us
  other arithmetic: 24 us -> 0.08 us
  blocking collectives: 37 us -> 23.9 us
  between operations: 13 us -> 0.77 us
  matrix products: 10.5 us -> 0 us
  waiting for transfers between devices: 29.1 us -> 19.7 us
  starting transfers between devices: 26.6 us -> 29.8 us
    all_gather x4 -> x0, blocking collectives: 37 us -> none  [collected_together(): both, at, found = (lax.all_gather(jnp.concatenate(lines), axis), 0, {})]
    pallas_call x0 -> x9, Pallas kernels: none -> 34.3 us  [call(): pl.pallas_call(body, out_shape=[jax.ShapeDtypeStruct(*o) for o in out], i...]
    all_to_all x0 -> x2, blocking collectives: none -> 23.9 us  [handed(): return lax.all_to_all(x, axis, 0, 0, tiled=True)]
    slice x19 -> x0, local copies, waits for them, and re-layouts: 14.4 us -> none  [the longest x4 4.01 us: line_solve(): lax.slice_in_dim(local_part, 0, 2, axis=line_axis)]
    all_to_all x3, waiting for transfers between devices: 29.1 us -> 15.1 us  [handed(): return lax.all_to_all(x, axis, 0, 0, tiled=True)]
    reduce_sum x5 -> x0, other arithmetic: 10.6 us -> none  [the longest x1 9.21 us: shards(): local_sums = jnp.sum(residual * residual, axis=(1, 2, 3))]
    dot_general x6 -> x0, matrix products: 10.5 us -> none  [the longest x3 6.31 us: line_solve(): jnp.einsum(patterns[line_axis], inverse, line_field, precision=exact_mode)]
    reshape x7 -> x0, local copies, waits for them, and re-layouts: 6.45 us -> none  [the longest x3 5.79 us: in_order(): parts.reshape(*dims[:dim], dims[dim] * dims[dim + 1], *dims[dim + 2:])]
  transfers between devices with their start and end apart: 9 -> 12, of which waited for: 1 -> 6; matrix products, arithmetic and copies ran while one was open for 15% -> 0% of each run, Pallas kernels for 0% -> 10%
where the time goes in v1:
time: 127 us; the launch traced here: 125 us
  Pallas kernels  34.3 us (27%)
  starting transfers between devices  29.8 us (23%)
  blocking collectives  23.9 us (19%)
  waiting for transfers between devices  19.7 us (16%)
  local copies, waits for them, and re-layouts  16.1 us (13%)
    pallas_call x9, Pallas kernels, call(): pl.pallas_call(body, out_shape=[jax.ShapeDtypeStruct(*o) for o in out], i...  34.3 us
    all_to_all x2, blocking collectives, handed(): return lax.all_to_all(x, axis, 0, 0, tiled=True)  23.9 us
    ppermute x9, starting transfers between devices, shifted(): return lax.ppermute(x, axis, [(i, (i + by) % size) for i in range(size)])  16.2 us
    unnamed x46, local copies, waits for them, and re-layouts  15.6 us
    all_to_all x3, waiting for transfers between devices, handed(): return lax.all_to_all(x, axis, 0, 0, tiled=True)  15.1 us
    all_to_all x3, starting transfers between devices, handed(): return lax.all_to_all(x, axis, 0, 0, tiled=True)  13.6 us
    ppermute x9, waiting for transfers between devices, shifted(): return lax.ppermute(x, axis, [(i, (i + by) % size) for i in range(size)])  4.53 us
  transfers between devices with their start and end apart: 12, of which 6 were waited for; matrix products, arithmetic and copies ran while one was open for 0% of the time, Pallas kernels for 10%

profile of v1, /device:TPU:2, one launch (start us, length us, event | category | flops | bytes accessed | tf_op | source)
XLA Modules:
  0.0 124.6 jit_solution(10618045915889221020)
XLA Ops:
  0.6 1.3 %copy-done = f32[5,32,16,128]{3,2,1,0:T(8,128)S(1)} copy-done((f32[5,32,16,128]{3,2,1,0:T(8,128)S(1)}, f32[5,32,16,128]{3,2,1,0:T(8,128)}, u32[]{:S(2)}) %copy-start) | copy-done | bytes 1310744
  1.9 1.5 %shard_map.95 = (f32[16,512]{1,0:T(8,128)S(1)}, f32[16,512]{1,0:T(8,128)S(1)}, f32[320,128]{1,0:T(8,128)}, f32[320,128]{1,0:T(8,128)}, f32[160,128]{1,0:T(8,128)}, /*index=5*/f32[160,128]{1,0:T(8,128)}) custom-call(f32[2560,128]{1,0:T(8,128)S(1)} %bitcast.17), custom_call_target="tpu_custom_call" | custom-call | flops 1000000 | bytes 1310720 | tf_op jit(solution)/shard_map/pallas_call | solution.py:45
  3.5 1.7 %collective-permute-start.3 = (f32[320,128]{1,0:T(8,128)}, f32[320,128]{1,0:T(8,128)S(1)}, u32[]{:S(2)}, u32[]{:S(2)}) collective-permute-start(f32[320,128]{1,0:T(8,128)} %get-tuple-element.31), channel_id=1, source_target_pairs={{0,56},{8,0},{16,8},{24,16},{32,24},{40,32},{48,40},{56,48},{1,57}... | collective-permute-start | bytes 491528 | tf_op jit(solution)/shard_map/ppermute | solution.py:465
  5.2 1.6 %collective-permute-start = (f32[16,512]{1,0:T(8,128)S(1)}, f32[16,512]{1,0:T(8,128)S(1)}, u32[]{:S(2)}, u32[]{:S(2)}) collective-permute-start(f32[16,512]{1,0:T(8,128)S(1)} %get-tuple-element.28.own_hi), channel_id=1, source_target_pairs={{0,64},{64,128},{128,192},{192,0},{1,65},{65,129},{129,193},{193,1... | collective-permute-start | bytes 98312 | tf_op jit(solution)/shard_map/ppermute | solution.py:465
  6.8 1.7 %collective-permute-start.1 = (f32[16,512]{1,0:T(8,128)S(1)}, f32[16,512]{1,0:T(8,128)}, u32[]{:S(2)}, u32[]{:S(2)}) collective-permute-start(f32[16,512]{1,0:T(8,128)S(1)} %get-tuple-element.29.own_lo), channel_id=1, source_target_pairs={{0,192},{64,0},{128,64},{192,128},{1,193},{65,1},{129,65},{193,129... | collective-permute-start | bytes 98312 | tf_op jit(solution)/shard_map/ppermute | solution.py:465
  8.4 1.9 %collective-permute-start.4 = (f32[160,128]{1,0:T(8,128)}, f32[160,128]{1,0:T(8,128)S(1)}, u32[]{:S(2)}, u32[]{:S(2)}) collective-permute-start(f32[160,128]{1,0:T(8,128)} %get-tuple-element.32), channel_id=1, source_target_pairs={{0,1},{1,2},{2,3},{3,4},{4,5},{5,6},{6,7},{7,0},{8,9},{9,10},{10,1... | collective-permute-start | bytes 245768 | tf_op jit(solution)/shard_map/ppermute | solution.py:465
  11.0 5.8 %collective-permute-start.5 = (f32[160,128]{1,0:T(8,128)}, f32[160,128]{1,0:T(8,128)S(1)}, u32[]{:S(2)}, u32[]{:S(2)}) collective-permute-start(f32[160,128]{1,0:T(8,128)} %get-tuple-element.33), channel_id=1, source_target_pairs={{0,7},{1,0},{2,1},{3,2},{4,3},{5,4},{6,5},{7,6},{8,15},{9,8},{10,9... | collective-permute-start | bytes 245768 | tf_op jit(solution)/shard_map/ppermute | solution.py:465
  22.7 7.9 %shard_map.96 = (bf16[10,128,128]{2,1,0:T(8,128)(2,1)S(1)}, bf16[10,128,128]{2,1,0:T(8,128)(2,1)S(1)}, bf16[10,128,128]{2,1,0:T(8,128)(2,1)S(1)}, bf16[10,512,12...) custom-call(f32[3,5]{1,0:T(4,128)S(1)} %copy-done.22, ...), custom_call_target="tpu_custom_call" | custom-call | flops 20000000 | bytes 399432 | tf_op jit(solution)/shard_map/pallas_call | solution.py:45
  33.1 13.0 %shard_map.97 = (f32[2560,128]{1,0:T(8,128)S(1)}, f32[24,512]{1,0:T(8,128)S(1)}) custom-call(f32[2560,128]{1,0:T(8,128)S(1)} %bitcast.18, f32[16,512]{1,0:T(8,128)S(1)} %copy-done.19, f32[16,512]{1,0:T(8,128)} %collective-permute-done.1.xhi, f32[320,128]{1,0:T(8,128)S(1)} %collective-permute-done.2.ylo, f32[320,128]{1,0:T(8,128)S(1)} %collective-permute-done.3.yhi, ...), custom_call_target="tpu_custom_call" | custom-call | flops 1000000 | bytes 3899392 | tf_op jit(solution)/shard_map/pallas_call | solution.py:45
  46.1 1.9 %collective-permute-start.8 = (f32[24,512]{1,0:T(8,128)S(1)}, f32[24,512]{1,0:T(8,128)S(1)}, u32[]{:S(2)}, u32[]{:S(2)}) collective-permute-start(f32[24,512]{1,0:T(8,128)S(1)} %get-tuple-element.38.b0), channel_id=1, source_target_pairs={{0,192},{64,0},{128,64},{192,128},{1,193},{65,1},{129,65},{193,129... | collective-permute-start | bytes 147464 | tf_op jit(solution)/shard_map/ppermute | solution.py:465
  50.2 3.3 %collective-permute-done.7.b2 = f32[24,512]{1,0:T(8,128)S(1)} collective-permute-done((f32[24,512]{1,0:T(8,128)S(1)}, f32[24,512]{1,0:T(8,128)S(1)}, u32[]{:S(2)}, u32[]{:S(2)}) %collective-permute-start.7) | collective-permute-done | bytes 49184 | tf_op jit(solution)/shard_map/ppermute | solution.py:465
  54.1 2.5 %shard_map.98 = (f32[2560,128]{1,0:T(8,128)S(1)}, f32[704,128]{1,0:T(8,128)S(1)}, f32[320,128]{1,0:T(8,128)}) custom-call(f32[2560,128]{1,0:T(8,128)S(1)} %get-tuple-element.37.w, f32[24,512]{1,0:T(8,128)S(1)} %get-tuple-element.38.b0, f32[24,512]{1,0:T(8,128)S(1)} %collective-permute-done.6.b1, f32[24,512]{1,0:T(8,128)S(1)} %collective-permute-done.7.b2, ...), custom_call_target="tpu_custom_call" | custom-call | flops 1000000 | bytes 1851392 | tf_op jit(solution)/shard_map/pallas_call | solution.py:45
  57.6 11.7 %all_to_all.55 = f32[8,88,128]{2,1,0:T(8,128)S(1)} all-to-all(f32[8,88,128]{2,1,0:T(8,128)S(1)} %bitcast.25), channel_id=1, replica_groups=mesh['gx'=4,'gy'=8,'gz'=8] {'gy'}, dimensions={0} | all-to-all | bytes 720896 | tf_op jit(solution)/shard_map/all_to_all | solution.py:460
  69.4 4.0 %all-to-all-start = ((f32[8,40,128]{2,1,0:T(8,128)}), f32[8,40,128]{2,1,0:T(8,128)S(1)}, u32[]{:S(2)}, u32[]{:S(2)}) async-start(f32[8,40,128]{2,1,0:T(8,128)} %bitcast.4), calls=%async_computation | async-start | bytes 327680 | tf_op jit(solution)/shard_map/all_to_all | solution.py:460
  73.3 1.6 %shard_map.99 = (f32[640,128]{1,0:T(8,128)}, f32[8,128]{1,0:T(8,128)S(1)}) custom-call(f32[704,128]{1,0:T(8,128)S(1)} %bitcast.19, bf16[10,128,128]{2,1,0:T(8,128)(2,1)S(1)} %get-tuple-element.44.my), custom_call_target="tpu_custom_call" | custom-call | flops 1000000 | bytes 688128 | tf_op jit(solution)/shard_map/pallas_call | solution.py:45
  74.9 8.0 %all-to-all-done = f32[8,40,128]{2,1,0:T(8,128)S(1)} async-done(((f32[8,40,128]{2,1,0:T(8,128)}), f32[8,40,128]{2,1,0:T(8,128)S(1)}, u32[]{:S(2)}, u32[]{:S(2)}) %all-to-all-start) | async-done | bytes 163872 | tf_op jit(solution)/shard_map/all_to_all | solution.py:460
  83.7 12.2 %all_to_all.56 = f32[8,48,128]{2,1,0:T(8,128)S(1)} all-to-all(f32[8,48,128]{2,1,0:T(8,128)S(1)} %bitcast.23), channel_id=1, replica_groups=mesh['gx'=4,'gy'=8,'gz'=8] {'gz'}, dimensions={0} | all-to-all | bytes 393216 | tf_op jit(solution)/shard_map/all_to_all | solution.py:460
  95.8 4.8 %all-to-all-start.3 = ((f32[8,80,128]{2,1,0:T(8,128)}), f32[8,80,128]{2,1,0:T(8,128)S(1)}, u32[]{:S(2)}, u32[]{:S(2)}) async-start(f32[8,80,128]{2,1,0:T(8,128)} %bitcast.10), calls=%async_computation.3 | async-start | bytes 655360 | tf_op jit(solution)/shard_map/all_to_all | solution.py:460
  101.4 6.0 %all-to-all-done.3 = f32[8,80,128]{2,1,0:T(8,128)S(1)} async-done(((f32[8,80,128]{2,1,0:T(8,128)}), f32[8,80,128]{2,1,0:T(8,128)S(1)}, u32[]{:S(2)}, u32[]{:S(2)}) %all-to-all-start.3) | async-done | bytes 327712 | tf_op jit(solution)/shard_map/all_to_all | solution.py:460
  107.4 4.8 %all-to-all-start.4 = ((f32[8,80,128]{2,1,0:T(8,128)}), f32[8,80,128]{2,1,0:T(8,128)S(1)}, u32[]{:S(2)}, u32[]{:S(2)}) async-start(f32[8,80,128]{2,1,0:T(8,128)} %bitcast.12), calls=%async_computation.4 | async-start | bytes 655360 | tf_op jit(solution)/shard_map/all_to_all | solution.py:460
  113.2 1.3 %copy-done.5 = f32[2560,128]{1,0:T(8,128)S(1)} copy-done((f32[2560,128]{1,0:T(8,128)S(1)}, f32[2560,128]{1,0:T(8,128)}, u32[]{:S(2)}) %copy-start.5) | copy-done | bytes 1310744
  115.6 1.7 %shard_map.102.v2 = f32[2560,128]{1,0:T(8,128)S(1)} custom-call(f32[2560,128]{1,0:T(8,128)S(1)} %copy-done.5, f32[320,128]{1,0:T(8,128)S(1)} %get-tuple-element.47.zc, f32[640,128]{1,0:T(8,128)S(1)} %bitcast.21, bf16[10,256,32]{2,1,0:T(8,128)(2,1)S(1)} %copy-done.7, bf16[10,512,128]{2,1,0:T(8,128)(2,1)S(1)} %get-tuple-element.50.qy), custom_call_target="tpu_custom_call" | custom-call | flops 1000000 | bytes 3276800 | tf_op jit(solution)/shard_map/pallas_call | solution.py:45
  117.9 1.1 all-to-all-done.4
  120.0 4.6 %shard_map.103 = f32[2560,128]{1,0:T(8,128)} custom-call(s32[3]{0:T(128)S(1)} %copy-done.21, f32[2560,128]{1,0:T(8,128)S(1)} %shard_map.102.v2, f32[640,128]{1,0:T(8,128)S(1)} %bitcast.20, f32[8,128]{1,0:T(8,128)S(1)} %get-tuple-element.52.fin, bf16[10,128,128]{2,1,0:T(8,128)(2,1)S(1)} %get-tuple-element.44.my, bf16[10,128,16]{2,1,0:T(8,128)(2,1)S(1)} %copy-done.9, ...), custom_call_target="tpu_custom_call" | custom-call | flops 1000000 | bytes 3321868 | tf_op jit(solution)/shard_map/pallas_call | solution.py:45
  (59 shorter events, 17.8 us)
Async XLA Ops:
  0.6 1.3 %copy-start = (f32[5,32,16,128]{3,2,1,0:T(8,128)S(1)}, f32[5,32,16,128]{3,2,1,0:T(8,128)}, u32[]{:S(2)}) copy-start(f32[5,32,16,128]{3,2,1,0:T(8,128)} %param.8) | copy-start | bytes 3932164
  1.9 29.6 %copy-start.1 = (f32[5,32,16,128]{3,2,1,0:T(8,128)S(1)}, f32[5,32,16,128]{3,2,1,0:T(8,128)}, u32[]{:S(2)}) copy-start(f32[5,32,16,128]{3,2,1,0:T(8,128)} %param.8) | copy-start | bytes 3932164
  3.4 13.3 %copy-start.16 = (f32[16,512]{1,0:T(8,128)}, f32[16,512]{1,0:T(8,128)S(1)}, u32[]{:S(2)}) copy-start(f32[16,512]{1,0:T(8,128)S(1)} %get-tuple-element.28.own_hi) | copy-start | bytes 98308
  3.5 28.1 %collective-permute-start.2 = (f32[320,128]{1,0:T(8,128)}, f32[320,128]{1,0:T(8,128)S(1)}, u32[]{:S(2)}, u32[]{:S(2)}) collective-permute-start(f32[320,128]{1,0:T(8,128)} %get-tuple-element.30), channel_id=1, source_target_pairs={{0,8},{8,16},{16,24},{24,32},{32,40},{40,48},{48,56},{56,0},{1,9},... | collective-permute-start | bytes 491528 | tf_op jit(solution)/shard_map/ppermute | solution.py:465
  3.5 28.1 %collective-permute-start.3 = (f32[320,128]{1,0:T(8,128)}, f32[320,128]{1,0:T(8,128)S(1)}, u32[]{:S(2)}, u32[]{:S(2)}) collective-permute-start(f32[320,128]{1,0:T(8,128)} %get-tuple-element.31), channel_id=1, source_target_pairs={{0,56},{8,0},{16,8},{24,16},{32,24},{40,32},{48,40},{56,48},{1,57}... | collective-permute-start | bytes 491528 | tf_op jit(solution)/shard_map/ppermute | solution.py:465
  5.2 5.2 %collective-permute-start = (f32[16,512]{1,0:T(8,128)S(1)}, f32[16,512]{1,0:T(8,128)S(1)}, u32[]{:S(2)}, u32[]{:S(2)}) collective-permute-start(f32[16,512]{1,0:T(8,128)S(1)} %get-tuple-element.28.own_hi), channel_id=1, source_target_pairs={{0,64},{64,128},{128,192},{192,0},{1,65},{65,129},{129,193},{193,1... | collective-permute-start | bytes 98312 | tf_op jit(solution)/shard_map/ppermute | solution.py:465
  6.8 24.7 %collective-permute-start.1 = (f32[16,512]{1,0:T(8,128)S(1)}, f32[16,512]{1,0:T(8,128)}, u32[]{:S(2)}, u32[]{:S(2)}) collective-permute-start(f32[16,512]{1,0:T(8,128)S(1)} %get-tuple-element.29.own_lo), channel_id=1, source_target_pairs={{0,192},{64,0},{128,64},{192,128},{1,193},{65,1},{129,65},{193,129... | collective-permute-start | bytes 98312 | tf_op jit(solution)/shard_map/ppermute | solution.py:465
  8.4 23.1 %collective-permute-start.4 = (f32[160,128]{1,0:T(8,128)}, f32[160,128]{1,0:T(8,128)S(1)}, u32[]{:S(2)}, u32[]{:S(2)}) collective-permute-start(f32[160,128]{1,0:T(8,128)} %get-tuple-element.32), channel_id=1, source_target_pairs={{0,1},{1,2},{2,3},{3,4},{4,5},{5,6},{6,7},{7,0},{8,9},{9,10},{10,1... | collective-permute-start | bytes 245768 | tf_op jit(solution)/shard_map/ppermute | solution.py:465
  11.0 20.6 %collective-permute-start.5 = (f32[160,128]{1,0:T(8,128)}, f32[160,128]{1,0:T(8,128)S(1)}, u32[]{:S(2)}, u32[]{:S(2)}) collective-permute-start(f32[160,128]{1,0:T(8,128)} %get-tuple-element.33), channel_id=1, source_target_pairs={{0,7},{1,0},{2,1},{3,2},{4,3},{5,4},{6,5},{7,6},{8,15},{9,8},{10,9... | collective-permute-start | bytes 245768 | tf_op jit(solution)/shard_map/ppermute | solution.py:465
  16.9 1.0 copy-start.10
  22.7 23.3 %copy-start.20 = (s32[3]{0:T(128)}, s32[3]{0:T(128)S(1)}, u32[]{:S(2)}) copy-start(s32[3]{0:T(128)S(1)} %pad_add_fusion.idx) | copy-start | bytes 40
  31.5 14.6 %copy-start.8 = (bf16[10,128,16]{2,1,0:T(8,128)(2,1)}, bf16[10,128,16]{2,1,0:T(8,128)(2,1)S(1)}, u32[]{:S(2)}) copy-start(bf16[10,128,16]{2,1,0:T(8,128)(2,1)S(1)} %get-tuple-element.53.qzy) | copy-start | bytes 122884
  46.1 4.2 %collective-permute-start.8 = (f32[24,512]{1,0:T(8,128)S(1)}, f32[24,512]{1,0:T(8,128)S(1)}, u32[]{:S(2)}, u32[]{:S(2)}) collective-permute-start(f32[24,512]{1,0:T(8,128)S(1)} %get-tuple-element.38.b0), channel_id=1, source_target_pairs={{0,192},{64,0},{128,64},{192,128},{1,193},{65,1},{129,65},{193,129... | collective-permute-start | bytes 147464 | tf_op jit(solution)/shard_map/ppermute | solution.py:465
  48.0 5.6 %collective-permute-start.7 = (f32[24,512]{1,0:T(8,128)S(1)}, f32[24,512]{1,0:T(8,128)S(1)}, u32[]{:S(2)}, u32[]{:S(2)}) collective-permute-start(f32[24,512]{1,0:T(8,128)S(1)} %get-tuple-element.38.b0), channel_id=1, source_target_pairs={{0,128},{64,192},{128,0},{192,64},{1,129},{65,193},{129,1},{193,65... | collective-permute-start | bytes 147464 | tf_op jit(solution)/shard_map/ppermute | solution.py:465
  48.6 5.5 %collective-permute-start.6 = (f32[24,512]{1,0:T(8,128)S(1)}, f32[24,512]{1,0:T(8,128)S(1)}, u32[]{:S(2)}, u32[]{:S(2)}) collective-permute-start(f32[24,512]{1,0:T(8,128)S(1)} %get-tuple-element.38.b0), channel_id=1, source_target_pairs={{0,64},{64,128},{128,192},{192,0},{1,65},{65,129},{129,193},{193,1... | collective-permute-start | bytes 147464 | tf_op jit(solution)/shard_map/ppermute | solution.py:465
  56.6 1.1 copy-start.4
  69.4 13.6 %all-to-all-start = ((f32[8,40,128]{2,1,0:T(8,128)}), f32[8,40,128]{2,1,0:T(8,128)S(1)}, u32[]{:S(2)}, u32[]{:S(2)}) async-start(f32[8,40,128]{2,1,0:T(8,128)} %bitcast.4), calls=%async_computation | async-start | bytes 327680 | tf_op jit(solution)/shard_map/all_to_all | solution.py:460
  95.8 11.6 %all-to-all-start.3 = ((f32[8,80,128]{2,1,0:T(8,128)}), f32[8,80,128]{2,1,0:T(8,128)S(1)}, u32[]{:S(2)}, u32[]{:S(2)}) async-start(f32[8,80,128]{2,1,0:T(8,128)} %bitcast.10), calls=%async_computation.3 | async-start | bytes 655360 | tf_op jit(solution)/shard_map/all_to_all | solution.py:460
  107.4 4.8 %copy-start.2 = (f32[8,80,128]{2,1,0:T(8,128)}, f32[8,80,128]{2,1,0:T(8,128)S(1)}, u32[]{:S(2)}) copy-start(f32[8,80,128]{2,1,0:T(8,128)S(1)} %all-to-all-done.3) | copy-start | bytes 983044
  107.4 11.6 %all-to-all-start.4 = ((f32[8,80,128]{2,1,0:T(8,128)}), f32[8,80,128]{2,1,0:T(8,128)S(1)}, u32[]{:S(2)}, u32[]{:S(2)}) async-start(f32[8,80,128]{2,1,0:T(8,128)} %bitcast.12), calls=%async_computation.4 | async-start | bytes 655360 | tf_op jit(solution)/shard_map/all_to_all | solution.py:460
  113.2 1.3 %copy-start.5 = (f32[2560,128]{1,0:T(8,128)S(1)}, f32[2560,128]{1,0:T(8,128)}, u32[]{:S(2)}) copy-start(f32[2560,128]{1,0:T(8,128)} %copy-done.4) | copy-start | bytes 3932164
  114.5 1.1 copy-start.7
  115.6 3.4 %copy-start.21 = (s32[3]{0:T(128)S(1)}, s32[3]{0:T(128)}, u32[]{:S(2)}) copy-start(s32[3]{0:T(128)} %copy-done.20) | copy-start | bytes 40
  119.0 1.0 copy-start.9
  (11 other events, 8.9 us)
